TPU v7x, 32 devices: a whole 2x2x4 slice. The times are simulated.
32 devices in a mesh: blk: 16 (over z, y, core), rhs: 2 (over x).
Axes of the slice: x: 2, y: 2, z: 4, core: 2. Of those that a mesh axis runs over, the one named last changes fastest.
Arguments:
- signal: bfloat16 [131072, 256], P('blk', 'rhs'), may hold values from -6 to 6
- col_factor: bfloat16 [96, 131072], P(None, 'blk'), may hold values from -0.5 to 0.5
- row_factor: bfloat16 [96, 131072], P(None, 'blk'), may hold values from -0.625 to 0.625
- level_factor: bfloat16 [4, 16, 2, 64, 48, 192], P(None, 'blk', None, 'rhs'), may hold values from -0.4375 to 0.4375
- col_leaf_sizes: int32 [16, 128], P('blk'), may hold values from 1 to 128, 8192 in all within a row
- row_leaf_sizes: int32 [16, 128], P('blk'), may hold values from 1 to 128, 8192 in all within a row
- level_order: int32 [4, 16, 128], P(None, 'blk'), may hold values from 0 to 127, each once within a row
Outputs:
- result: bfloat16 [131072, 256], P('blk', 'rhs')
Inputs may be any that keep to these rules, and one draw needn't show every extreme that they name: `col_leaf_sizes`: row d lists in order the sizes of the 128 column leaves that cover unknowns d * 8192 to (d + 1) * 8192 - 1; each row sums to 8192 and its largest entry is 128. `row_leaf_sizes`: row d lists in order the sizes of the 128 row leaves that cover unknowns d * 8192 to (d + 1) * 8192 - 1; each row sums to 8192 and its largest entry is 128. Every level_order[l, d, :] is a permutation of 0 to 127.
All inputs are finite; a program needn't handle non-finite values.
Results may differ from a plain program's by a relative error of at most 0.0076.
Values may be sent and summed in bfloat16 or wider, within the bound.
A program may use at most 128 MiB of HBM per device.

v0:
```python
import functools

import jax
import jax.numpy as jnp
from jax import lax
from jax.experimental import pallas as pl
from jax.experimental.pallas import tpu as pltpu
from jax.sharding import PartitionSpec as P

LANES = 128
ROWS = 16
MESH = pl.DeviceIdType.MESH


def turn(values):
    half = values.shape[-1] // 2
    return jnp.concatenate([-values[:, half:], values[:, :half]], axis=1)


def levels_kernel(
    n, order, first_hbm, lf_hbm, rf_hbm, coef, flipped,
    head, tail, loose, rf, send, arr,
    load_sem, w_send, w_recv, a_send, a_recv,
):
    levels, _, _, depth, rank, _ = head.shape
    width = LANES + loose.shape[-1]
    blocks = coef.shape[0]
    points = rf.shape[1]
    per = blocks // n
    half = n // 2
    sources = n // 4
    me = lax.axis_index("blk")
    col = lax.axis_index("rhs")
    side = me // half
    place = lax.rem(me, half)

    def loads(l):
        return (
            pltpu.make_async_copy(
                lf_hbm.at[l, :, :, :, pl.ds(0, LANES)], head.at[l, col], load_sem.at[l, 0]
            ),
            pltpu.make_async_copy(
                lf_hbm.at[l, :, :, :, pl.ds(LANES, width - LANES)], loose.at[l], load_sem.at[l, 1]
            ),
        )

    load_coef = pltpu.make_async_copy(first_hbm, coef, load_sem.at[levels, 0])
    load_rows = pltpu.make_async_copy(rf_hbm, rf, load_sem.at[levels, 1])
    load_coef.start()
    for l in range(levels):
        for copy in loads(l):
            copy.start()
    load_rows.start()

    barrier = pltpu.get_barrier_semaphore()

    def greet(k, carry):
        peer = lax.rem(me + k, n)
        pl.semaphore_signal(barrier, inc=1, device_id=(peer, col), device_id_type=MESH)
        return carry

    lax.fori_loop(1, n, greet, 0)
    pl.semaphore_signal(barrier, inc=1, device_id=(me, 1 - col), device_id_type=MESH)

    def weight_copies(l, owner):
        return [
            pltpu.make_async_remote_copy(
                src_ref=ref.at[l, owner],
                dst_ref=ref.at[l, owner],
                send_sem=w_send.at[l, at],
                recv_sem=w_recv.at[l, at],
                device_id=(me, 1 - col),
                device_id_type=MESH,
            )
            for at, ref in enumerate((head, tail))
        ]

    def pack(l):
        def one(i, carry):
            tail[l, col, i] = jnp.concatenate([loose[l, 0, i], loose[l, 1, i]], axis=1)
            return carry

        lax.fori_loop(0, depth, one, 0, unroll=4)

    def block_copy(par, peer):
        return pltpu.make_async_remote_copy(
            src_ref=send.at[peer],
            dst_ref=arr.at[par, me],
            send_sem=a_send.at[peer],
            recv_sem=a_recv.at[par, me],
            device_id=(peer, col),
            device_id_type=MESH,
        )

    def arrival(par, source):
        return pltpu.make_async_remote_copy(
            src_ref=send.at[source],
            dst_ref=arr.at[par, source],
            send_sem=a_send.at[source],
            recv_sem=a_recv.at[par, source],
            device_id=(source, col),
            device_id_type=MESH,
        )

    def across(k):
        return (1 - side) * half + lax.rem(place + k, half)

    def beside(k):
        return side * half + lax.rem(place + k, half)

    blank = jnp.zeros((2 * LANES - width, LANES), jnp.bfloat16)

    load_coef.wait()
    pl.semaphore_wait(barrier, n)

    def level(l, carry):
        par = lax.rem(l, 2)

        def choose(peer):
            for q in range(per):
                send[peer, q] = coef[order[l, peer * per + q]]

        def hand_out(k, inner):
            choose(across(k))
            block_copy(par, across(k)).start()

            @pl.when(k > 0)
            def _():
                choose(beside(k))
                block_copy(par, beside(k)).start()

            return inner

        lax.fori_loop(0, half, hand_out, 0)
        choose(me)
        pltpu.make_async_copy(send.at[me], arr.at[par, me], a_recv.at[par, me]).start()

        @pl.when(l == 0)
        def _():
            for later in range(levels):
                for copy in loads(later):
                    copy.wait()
                pack(later)
                for copy in weight_copies(later, col):
                    copy.start()
            load_rows.wait()

            def flip(c, inner):
                base = pl.multiple_of(c * LANES, LANES)
                flipped[pl.ds(base, LANES), :] = rf[:, pl.ds(base, LANES)].T
                return inner

            lax.fori_loop(0, points // LANES, flip, 0, unroll=4)

        for copy in weight_copies(l, 1 - col):
            copy.wait_recv()

        def combine(k, inner):
            s = lax.rem(place + half - k, half)
            owner = s // sources
            at = lax.rem(s, sources) * per
            arrival(par, s).wait_recv()
            arrival(par, s + half).wait_recv()
            for q in range(per):
                i = at + q
                x = arr[par, s, q]
                y = arr[par, s + half, q]
                jx = turn(x)
                jy = turn(y)
                rest = tail[l, owner, i]
                upper = jnp.concatenate([head[l, owner, 0, i], rest], axis=1)
                lower = jnp.concatenate([head[l, owner, 1, i], rest], axis=1)
                cut = LANES - 2 * rank
                over = jnp.concatenate([x, jx, y, jy, blank], axis=0)
                under = jnp.concatenate([y, jy, x[:cut], blank, x[cut:], jx], axis=0)
                coef[s * per + q] = jnp.dot(
                    upper, over, preferred_element_type=jnp.float32
                ).astype(jnp.bfloat16)
                coef[(s + half) * per + q] = jnp.dot(
                    lower, under, preferred_element_type=jnp.float32
                ).astype(jnp.bfloat16)
            return inner

        lax.fori_loop(0, half, combine, 0)

        def sent(k, inner):
            block_copy(par, lax.rem(me + k, n)).wait_send()
            return inner

        lax.fori_loop(1, n, sent, 0)
        return carry

    lax.fori_loop(0, levels, level, 0)
    for l in range(levels):
        for copy in weight_copies(l, col):
            copy.wait_send()


def leaves_kernel(sizes, sig, cf, coef):
    blocks, rank, _ = coef.shape
    points = sig.shape[0]
    window = 2 * LANES
    lane = lax.broadcasted_iota(jnp.int32, (1, window), 1)

    def leaf(b, start):
        end = start + sizes[0, b]
        base = jnp.minimum(start // LANES * LANES, points - window)
        base = pl.multiple_of(base, LANES)
        inside = jnp.logical_and(lane >= start - base, lane < end - base)
        keep = jnp.where(inside, 1.0, 0.0).astype(jnp.bfloat16)
        weights = cf[:, pl.ds(base, window)] * keep
        sums = jnp.dot(weights, sig[pl.ds(base, window), :], preferred_element_type=jnp.float32)
        coef[b] = (sums[:rank] + turn(sums[rank:])).astype(jnp.bfloat16)
        return end

    lax.fori_loop(0, blocks, leaf, jnp.int32(0), unroll=8)


def rows_kernel(sizes, coef, flipped, out_hbm, out, sem):
    blocks, rank, _ = coef.shape
    points = out_hbm.shape[0]
    window = LANES + ROWS
    row = lax.broadcasted_iota(jnp.int32, (ROWS, LANES), 0)

    def leaf(b, start):
        base = pl.multiple_of(start // ROWS * ROWS, ROWS)
        values = coef[b]
        pair = jnp.concatenate([values, turn(values)], axis=0)
        sums = jnp.dot(flipped[pl.ds(base, window), :], pair, preferred_element_type=jnp.float32)
        before = out[pl.ds(base, ROWS), :].astype(jnp.float32)
        top = jnp.where(row < start - base, before, sums[:ROWS])
        out[pl.ds(base, ROWS), :] = top.astype(jnp.bfloat16)
        out[pl.ds(base + ROWS, LANES), :] = sums[ROWS:].astype(jnp.bfloat16)
        return start + sizes[0, b]

    lax.fori_loop(0, blocks, leaf, jnp.int32(0), unroll=8)
    copy = pltpu.make_async_copy(out.at[pl.ds(0, points)], out_hbm, sem)
    copy.start()
    copy.wait()


def local(
    n, signal, col_factor, row_factor, level_factor, col_leaf_sizes, row_leaf_sizes, level_order
):
    levels, _, halves, depth, rank, width = level_factor.shape
    blocks = col_leaf_sizes.shape[1]
    points, columns = signal.shape
    bf16 = jnp.bfloat16
    smem = pl.BlockSpec(memory_space=pltpu.SMEM)
    vmem = pl.BlockSpec(memory_space=pltpu.VMEM)
    anywhere = pl.BlockSpec(memory_space=pl.ANY)
    first = pl.pallas_call(
        leaves_kernel,
        out_shape=jax.ShapeDtypeStruct((blocks, row_factor.shape[0] // 2, columns), bf16),
        in_specs=[smem, vmem, vmem],
        out_specs=vmem,
        compiler_params=pltpu.CompilerParams(vmem_limit_bytes=32 << 20),
        name="leaves",
    )(col_leaf_sizes, signal, col_factor)
    factors = level_factor.reshape(levels, halves, depth, rank, width)
    coefficients, flipped = pl.pallas_call(
        functools.partial(levels_kernel, n),
        out_shape=(
            jax.ShapeDtypeStruct((blocks, rank, columns), bf16),
            jax.ShapeDtypeStruct((points + LANES + ROWS, 2 * rank), bf16),
        ),
        in_specs=[smem, anywhere, anywhere, anywhere],
        out_specs=(vmem, vmem),
        scratch_shapes=[
            pltpu.VMEM((levels, 2, halves, depth, rank, LANES), bf16),
            pltpu.VMEM((levels, 2, depth, rank, LANES), bf16),
            pltpu.VMEM((levels, halves, depth, rank, width - LANES), bf16),
            pltpu.VMEM((2 * rank, points), bf16),
            pltpu.VMEM((n, blocks // n, rank, columns), bf16),
            pltpu.VMEM((2, n, blocks // n, rank, columns), bf16),
            pltpu.SemaphoreType.DMA((levels + 1, 2)),
            pltpu.SemaphoreType.DMA((levels, 2)),
            pltpu.SemaphoreType.DMA((levels, 2)),
            pltpu.SemaphoreType.DMA((n,)),
            pltpu.SemaphoreType.DMA((2, n)),
        ],
        compiler_params=pltpu.CompilerParams(
            collective_id=0, has_side_effects=True, vmem_limit_bytes=48 << 20
        ),
        name="levels",
    )(level_order.reshape(levels, blocks), first, factors, row_factor)
    return pl.pallas_call(
        rows_kernel,
        out_shape=jax.ShapeDtypeStruct((points, columns), bf16),
        in_specs=[smem, vmem, vmem],
        out_specs=anywhere,
        scratch_shapes=[
            pltpu.VMEM((points + LANES + ROWS, columns), bf16),
            pltpu.SemaphoreType.DMA(()),
        ],
        compiler_params=pltpu.CompilerParams(vmem_limit_bytes=40 << 20),
        name="rows",
    )(row_leaf_sizes, coefficients, flipped)


def solution(mesh):
    in_specs = (
        P("blk", "rhs"),
        P(None, "blk"),
        P(None, "blk"),
        P(None, "blk", None, "rhs", None, None),
        P("blk", None),
        P("blk", None),
        P(None, "blk", None),
    )
    return jax.shard_map(
        functools.partial(local, mesh.shape["blk"]),
        mesh=mesh, in_specs=in_specs, out_specs=P("blk", "rhs"), check_vma=False,
    )
```

profile of v0, /device:TPU:0, one launch (start us, length us, event | category | flops | bytes accessed | tf_op | source)
XLA Modules:
  0.0 165.5 jit_solution(6600201641377261851)
XLA Ops:
  0.0 0.0 copy-start.1
  0.0 1.6 copy-done.1
  1.6 0.0 copy-start.3
  1.6 1.4 copy-done.3
  3.0 0.0 copy-start.5
  3.0 0.7 copy-done.5
  3.7 0.0 copy-start.2
  3.7 0.0 copy-start.4
  3.7 6.2 %leaves.1.first_hbm = bf16[128,48,128]{2,1,0:T(8,128)(2,1)S(1)} custom-call(s32[1,128]{1,0:T(1,128)S(1)} %copy-done.5, bf16[8192,128]{1,0:T(8,128)(2,1)S(1)} %copy-done.1, bf16[96,8192]{1,0:T(8,128)(2,1)S(1)} %copy-done.3), custom_call_target="tpu_custom_call" | custom-call | tf_op jit(solution)/shard_map/leaves/pallas_call | solution.py:252
  9.9 0.0 copy-done.2
  9.9 0.0 copy-done.4
  9.9 0.0 copy-start.6
  9.9 146.2 %levels.1 = (bf16[128,48,128]{2,1,0:T(8,128)(2,1)S(1)}, bf16[8336,96]{1,0:T(8,128)(2,1)}) custom-call(s32[4,128]{1,0:T(4,128)S(1)} %bitcast.2, bf16[128,48,128]{2,1,0:T(8,128)(2,1)S(1)} %leaves.1.first_hbm, bf16[4,2,32,48,192]{4,3,2,1,0:T(8,128)(2,1)} %bitcast.3, bf16[96,8192]{1,0:T(8,128)(2,1)S(1)} %copy-done.2), custom_call_target="tpu_custom_call" | custom-call | tf_op jit(solution)/shard_map/levels/pallas_call | solution.py:261
  156.1 0.0 copy-done.6
  156.1 0.0 copy-start
  156.1 1.6 copy-done
  157.7 7.8 %rows.1 = bf16[8192,128]{1,0:T(8,128)(2,1)} custom-call(s32[1,128]{1,0:T(1,128)S(1)} %copy-done.6, bf16[128,48,128]{2,1,0:T(8,128)(2,1)S(1)} %get-tuple-element.7.coef, bf16[8336,96]{1,0:T(8,128)(2,1)S(1)} %copy-done), custom_call_target="tpu_custom_call" | custom-call | tf_op jit(solution)/shard_map/rows/pallas_call | solution.py:287
Async XLA Ops:
  0.0 1.6 copy-start.1
  1.6 1.4 copy-start.3
  3.0 0.7 copy-start.5
  3.7 6.2 %copy-start.2 = (bf16[96,8192]{1,0:T(8,128)(2,1)S(1)}, bf16[96,8192]{1,0:T(8,128)(2,1)}, u32[]{:S(2)}) copy-start(bf16[96,8192]{1,0:T(8,128)(2,1)} %rf_hbm.1) | copy-start | bytes 4718596
  3.7 6.2 %copy-start.4 = (s32[4,1,128]{2,1,0:T(1,128)S(1)}, s32[4,1,128]{2,1,0:T(1,128)}, u32[]{:S(2)}) copy-start(s32[4,1,128]{2,1,0:T(1,128)} %param.13) | copy-start | bytes 6148
  9.9 146.2 %copy-start.6 = (s32[1,128]{1,0:T(1,128)S(1)}, s32[1,128]{1,0:T(1,128)}, u32[]{:S(2)}) copy-start(s32[1,128]{1,0:T(1,128)} %sizes.3) | copy-start | bytes 1540
  156.1 1.6 copy-start
where the time goes:
time: 166 us
  Pallas kernels  160 us (96%)
  local copies, waits for them, and re-layouts  5.26 us (3%)
    pallas_call x1, Pallas kernels, local(): pl.pallas_call(functools.partial(levels_kernel, n), out_shape=(jax.ShapeD...  146 us
    pallas_call x1, Pallas kernels, local(): pl.pallas_call(rows_kernel, out_shape=jax.ShapeDtypeStruct((points, colum...  7.81 us
    pallas_call x1, Pallas kernels, local(): pl.pallas_call(leaves_kernel, out_shape=jax.ShapeDtypeStruct((blocks, row...  6.21 us
    unnamed x14, local copies, waits for them, and re-layouts  5.26 us

commit v1 on v0

v1 whole, which is shorter than its diff:
```python
import functools

import jax
import jax.numpy as jnp
from jax import lax
from jax.experimental import pallas as pl
from jax.experimental.pallas import tpu as pltpu
from jax.sharding import PartitionSpec as P

LANES = 128
ROWS = 16
MESH = pl.DeviceIdType.MESH


def turn(values):
    half = values.shape[-1] // 2
    return jnp.concatenate([-values[:, half:], values[:, :half]], axis=1)


def main_kernel(
    n, sig_hbm, cf_hbm, rf_hbm, lf_hbm, col_sizes_hbm, row_sizes_hbm, order_hbm, leafwise,
    sig, cf, rf, flipped, head, tail, head_in, tail_in, loose, coef, send, arr,
    col_sizes, row_sizes, order, col_start, row_start,
    load_sem, cf_sem, small_sem, w_send, w_recv, a_send, a_recv,
):
    levels, _, depth, rank, _ = head.shape
    width = LANES + loose.shape[-1]
    blocks = coef.shape[0]
    chunks = sig.shape[0]
    per = blocks // n
    half = n // 2
    sources = n // 4
    me = lax.axis_index("blk")
    col = lax.axis_index("rhs")
    side = me // half
    place = lax.rem(me, half)
    bf16 = jnp.bfloat16

    smalls = [
        pltpu.make_async_copy(col_sizes_hbm, col_sizes, small_sem.at[0]),
        pltpu.make_async_copy(order_hbm, order, small_sem.at[1]),
        pltpu.make_async_copy(row_sizes_hbm, row_sizes, small_sem.at[2]),
    ]
    load_sig = pltpu.make_async_copy(sig_hbm, sig, load_sem.at[levels, 0])

    def load_cf(c):
        at = pl.ds(pl.multiple_of(c * LANES, LANES), LANES)
        return pltpu.make_async_copy(cf_hbm.at[:, at], cf.at[c], cf_sem.at[c])

    load_rf = pltpu.make_async_copy(rf_hbm, rf, load_sem.at[levels, 2])

    def loads(l):
        return (
            pltpu.make_async_copy(
                lf_hbm.at[l, :, :, :, pl.ds(0, LANES)], head.at[l], load_sem.at[l, 0]
            ),
            pltpu.make_async_copy(
                lf_hbm.at[l, :, :, :, pl.ds(LANES, width - LANES)], loose.at[l], load_sem.at[l, 1]
            ),
        )

    for copy in smalls:
        copy.start()
    load_sig.start()

    def start_cf(c, carry):
        load_cf(c).start()
        return carry

    lax.fori_loop(0, chunks, start_cf, 0)

    barrier = pltpu.get_barrier_semaphore()

    def greet(k, carry):
        peer = lax.rem(me + k, n)
        pl.semaphore_signal(barrier, inc=1, device_id=(peer, col), device_id_type=MESH)
        return carry

    lax.fori_loop(1, n, greet, 0)
    pl.semaphore_signal(barrier, inc=1, device_id=(me, 1 - col), device_id_type=MESH)

    for copy in smalls:
        copy.wait()

    def add_up(b, carry):
        first, last = carry
        col_start[b] = first
        row_start[b] = last
        return first + col_sizes[0, b], last + row_sizes[0, b]

    lax.fori_loop(0, blocks, add_up, (jnp.int32(0), jnp.int32(0)), unroll=8)

    def weight_copies(l):
        return [
            pltpu.make_async_remote_copy(
                src_ref=ref.at[l],
                dst_ref=into.at[l],
                send_sem=w_send.at[l, at],
                recv_sem=w_recv.at[l, at],
                device_id=(me, 1 - col),
                device_id_type=MESH,
            )
            for at, (ref, into) in enumerate(((head, head_in), (tail, tail_in)))
        ]

    def pack(l):
        def one(i, carry):
            tail[l, i] = jnp.concatenate([loose[l, 0, i], loose[l, 1, i]], axis=1)
            return carry

        lax.fori_loop(0, depth, one, 0, unroll=4)

    def block_copy(par, peer):
        return pltpu.make_async_remote_copy(
            src_ref=send.at[par, peer],
            dst_ref=arr.at[par, me],
            send_sem=a_send.at[par, peer],
            recv_sem=a_recv.at[par, me],
            device_id=(peer, col),
            device_id_type=MESH,
        )

    def arrival(par, source):
        return pltpu.make_async_remote_copy(
            src_ref=send.at[par, source],
            dst_ref=arr.at[par, source],
            send_sem=a_send.at[par, source],
            recv_sem=a_recv.at[par, source],
            device_id=(source, col),
            device_id_type=MESH,
        )

    def across(k):
        return (1 - side) * half + lax.rem(place + k, half)

    def beside(k):
        return side * half + lax.rem(place + k, half)

    def hand_out(par, choose):
        def one(k, inner):
            choose(across(k))
            block_copy(par, across(k)).start()

            @pl.when(k > 0)
            def _():
                choose(beside(k))
                block_copy(par, beside(k)).start()

            return inner

        lax.fori_loop(0, half, one, 0)
        choose(me)
        pltpu.make_async_copy(send.at[par, me], arr.at[par, me], a_recv.at[par, me]).start()

    def sent(par):
        def one(k, inner):
            block_copy(par, lax.rem(me + k, n)).wait_send()
            return inner

        lax.fori_loop(1, n, one, 0)

    window = 2 * LANES
    lane = lax.broadcasted_iota(jnp.int32, (1, window), 1)

    def leaves(peer):
        for q in range(per):
            b = order[0, peer * per + q]
            start = col_start[b]
            end = start + col_sizes[0, b]
            c = jnp.minimum(lax.div(start, LANES), chunks - 2)
            base = c * LANES
            inside = jnp.logical_and(lane >= start - base, lane < end - base)
            keep = jnp.where(inside, 1.0, 0.0).astype(bf16)
            weights = jnp.concatenate([cf[c], cf[c + 1]], axis=1) * keep
            values = jnp.concatenate([sig[c], sig[c + 1]], axis=0)
            sums = jnp.dot(weights, values, preferred_element_type=jnp.float32)
            send[0, peer, q] = (sums[:rank] + turn(sums[rank:])).astype(bf16)

    load_sig.wait()

    def wait_cf(c, carry):
        load_cf(c).wait()
        return carry

    lax.fori_loop(0, chunks, wait_cf, 0)
    for l in range(levels):
        for copy in loads(l):
            copy.start()
    load_rf.start()
    pl.semaphore_wait(barrier, n)
    hand_out(0, leaves)

    for l in range(levels):
        for copy in loads(l):
            copy.wait()
        pack(l)
        for copy in weight_copies(l):
            copy.start()
    load_rf.wait()

    def flip(c, inner):
        at = pl.ds(pl.multiple_of(c * LANES, LANES), LANES)
        rows = LANES // ROWS
        flipped[pl.ds(c * rows, rows)] = rf[:, at].T.reshape(rows, ROWS, 2 * rank)
        return inner

    lax.fori_loop(0, chunks, flip, 0, unroll=4)

    blank = jnp.zeros((2 * LANES - width, LANES), bf16)

    def combine(l, par, put):
        def pairs(owner, first, second):
            def one(k, inner):
                at = lax.rem(place + sources - k, sources)
                s = owner * sources + at
                arrival(par, s).wait_recv()
                arrival(par, s + half).wait_recv()
                for q in range(per):
                    i = at * per + q
                    x = arr[par, s, q]
                    y = arr[par, s + half, q]
                    jx = turn(x)
                    jy = turn(y)
                    rest = second[l, i]
                    upper = jnp.concatenate([first[l, 0, i], rest], axis=1)
                    lower = jnp.concatenate([first[l, 1, i], rest], axis=1)
                    cut = LANES - 2 * rank
                    over = jnp.concatenate([x, jx, y, jy, blank], axis=0)
                    under = jnp.concatenate([y, jy, x[:cut], blank, x[cut:], jx], axis=0)
                    put(s * per + q, jnp.dot(
                        upper, over, preferred_element_type=jnp.float32
                    ).astype(bf16))
                    put((s + half) * per + q, jnp.dot(
                        lower, under, preferred_element_type=jnp.float32
                    ).astype(bf16))
                return inner

            lax.fori_loop(0, sources, one, 0)

        pairs(col, head, tail)
        for copy in weight_copies(l):
            copy.wait_recv()
        pairs(1 - col, head_in, tail_in)

    def keep_block(b, values):
        coef[b] = values

    def level(l, carry):
        par = lax.rem(l, 2)
        combine(l, par, keep_block)

        @pl.when(l > 0)
        def _():
            sent(1 - par)

        def choose(peer):
            for q in range(per):
                send[1 - par, peer, q] = coef[order[l + 1, peer * per + q]]

        hand_out(1 - par, choose)
        return carry

    lax.fori_loop(0, levels - 1, level, 0)

    reach = leafwise.shape[1]

    def put_rows(b, values):
        base = lax.div(row_start[b], ROWS)
        rows = [flipped[base + i] for i in range(reach // ROWS)]
        pair = jnp.concatenate([values, turn(values)], axis=0)
        leafwise[b] = jnp.dot(
            jnp.concatenate(rows, axis=0), pair, preferred_element_type=jnp.float32
        ).astype(bf16)

    last = (levels - 1) % 2
    combine(levels - 1, last, put_rows)
    sent(1 - last)
    sent(last)
    for l in range(levels):
        for copy in weight_copies(l):
            copy.wait_send()


def rows_kernel(sizes, leafwise, out_hbm, out, sem):
    blocks, reach, _ = leafwise.shape
    points = out_hbm.shape[0]
    parts = sem.shape[0]
    chunk = points // parts
    group = 8
    row = lax.broadcasted_iota(jnp.int32, (ROWS, LANES), 0)

    def part(c):
        at = pl.ds(pl.multiple_of(c * chunk, chunk), chunk)
        return pltpu.make_async_copy(out.at[at], out_hbm.at[at], sem.at[c])

    def leaves(g, begin):
        start = begin
        for i in range(group):
            b = g * group + i
            base = pl.multiple_of(start // ROWS * ROWS, ROWS)
            before = out[pl.ds(base, ROWS), :]
            top = jnp.where(row < start - base, before, leafwise[b, pl.ds(0, ROWS), :])
            out[pl.ds(base, ROWS), :] = top
            out[pl.ds(base + ROWS, reach - ROWS), :] = leafwise[b, pl.ds(ROWS, reach - ROWS), :]
            start = start + sizes[0, b]

        return start

    lax.fori_loop(0, blocks // group, leaves, jnp.int32(0))
    for c in range(parts):
        part(c).start()
    for c in range(parts):
        part(c).wait()


def local(
    n, signal, col_factor, row_factor, level_factor, col_leaf_sizes, row_leaf_sizes, level_order
):
    levels, _, halves, depth, rank, width = level_factor.shape
    blocks = col_leaf_sizes.shape[1]
    points, columns = signal.shape
    per = blocks // n
    bf16 = jnp.bfloat16
    smem = pl.BlockSpec(memory_space=pltpu.SMEM)
    vmem = pl.BlockSpec(memory_space=pltpu.VMEM)
    hbm = pl.BlockSpec(memory_space=pltpu.HBM)
    reach = LANES + ROWS
    factors = level_factor.reshape(levels, halves, depth, rank, width)
    leafwise = pl.pallas_call(
        functools.partial(main_kernel, n),
        out_shape=pltpu.VMEM((blocks, reach, columns), bf16),
        in_specs=[hbm] * 7,
        out_specs=vmem,
        scratch_shapes=[
            pltpu.VMEM((points // LANES, LANES, columns), bf16),
            pltpu.VMEM((points // LANES, 2 * rank, LANES), bf16),
            pltpu.VMEM((2 * rank, points), bf16),
            pltpu.VMEM(((points + reach) // ROWS, ROWS, 2 * rank), bf16),
            pltpu.VMEM((levels, halves, depth, rank, LANES), bf16),
            pltpu.VMEM((levels, depth, rank, LANES), bf16),
            pltpu.VMEM((levels, halves, depth, rank, LANES), bf16),
            pltpu.VMEM((levels, depth, rank, LANES), bf16),
            pltpu.VMEM((levels, halves, depth, rank, width - LANES), bf16),
            pltpu.VMEM((blocks, rank, columns), bf16),
            pltpu.VMEM((2, n, per, rank, columns), bf16),
            pltpu.VMEM((2, n, per, rank, columns), bf16),
            pltpu.SMEM((1, blocks), jnp.int32),
            pltpu.SMEM((1, blocks), jnp.int32),
            pltpu.SMEM((levels, blocks), jnp.int32),
            pltpu.SMEM((blocks,), jnp.int32),
            pltpu.SMEM((blocks,), jnp.int32),
            pltpu.SemaphoreType.DMA((levels + 1, 3)),
            pltpu.SemaphoreType.DMA((points // LANES,)),
            pltpu.SemaphoreType.DMA((3,)),
            pltpu.SemaphoreType.DMA((levels, 2)),
            pltpu.SemaphoreType.DMA((levels, 2)),
            pltpu.SemaphoreType.DMA((2, n)),
            pltpu.SemaphoreType.DMA((2, n)),
        ],
        compiler_params=pltpu.CompilerParams(
            collective_id=0, has_side_effects=True, vmem_limit_bytes=58000000
        ),
        name="levels",
    )(
        signal.reshape(points // LANES, LANES, columns), col_factor, row_factor, factors, col_leaf_sizes, row_leaf_sizes,
        level_order.reshape(levels, blocks),
    )
    return pl.pallas_call(
        rows_kernel,
        out_shape=jax.ShapeDtypeStruct((points, columns), bf16),
        in_specs=[smem, vmem],
        out_specs=hbm,
        scratch_shapes=[
            pltpu.VMEM((points + reach, columns), bf16),
            pltpu.SemaphoreType.DMA((8,)),
        ],
        compiler_params=pltpu.CompilerParams(vmem_limit_bytes=16 << 20),
        name="rows",
    )(row_leaf_sizes, leafwise)


def solution(mesh):
    in_specs = (
        P("blk", "rhs"),
        P(None, "blk"),
        P(None, "blk"),
        P(None, "blk", None, "rhs", None, None),
        P("blk", None),
        P("blk", None),
        P(None, "blk", None),
    )
    return jax.shard_map(
        functools.partial(local, mesh.shape["blk"]),
        mesh=mesh, in_specs=in_specs, out_specs=P("blk", "rhs"), check_vma=False,
    )
```

time: 166 us -> 163 us (0.982)
  local copies, waits for them, and re-layouts: 5.26 us -> 0.01 us
  Pallas kernels: 160 us -> 162 us
    pallas_call x2 -> x1, Pallas kernels: 152 us -> 159 us  [local(): pl.pallas_call(functools.partial(main_kernel, n), out_shape=pltpu.VMEM((b...]
    unnamed x14 -> x2, local copies, waits for them, and re-layouts: 5.26 us -> 0.01 us
    pallas_call x1, Pallas kernels: 7.81 us -> 2.98 us  [local(): pl.pallas_call(rows_kernel, out_shape=jax.ShapeDtypeStruct((points, colum...]
where the time goes in v1:
time: 163 us; the launch traced here: 162 us
  Pallas kernels  162 us (99%)
    pallas_call x1, Pallas kernels, local(): pl.pallas_call(functools.partial(main_kernel, n), out_shape=pltpu.VMEM((b...  159 us

profile of v1, /device:TPU:0, one launch (start us, length us, event | category | flops | bytes accessed | tf_op | source)
XLA Modules:
  0.0 162.3 jit_solution(14514754740052201125)
XLA Ops:
  0.0 0.0 copy-start
  0.0 159.3 %levels.1.leafwise = bf16[128,144,128]{2,1,0:T(8,128)(2,1)S(1)} custom-call(bf16[64,128,128]{2,1,0:T(8,128)(2,1)} %bitcast.4, bf16[96,8192]{1,0:T(8,128)(2,1)} %cf_hbm.1, bf16[96,8192]{1,0:T(8,128)(2,1)} %rf_hbm.1, bf16[4,2,32,48,192]{4,3,2,1,0:T(8,128)(2,1)} %bitcast.3, s32[1,128]{1,0:T(1,128)} %col_sizes_hbm.1, s32[1,128]{1,0:T(1,128)} %sizes.1, ...), custom_call_target="tpu_custom_call" | custom-call | tf_op jit(solution)/shard_map/levels/pallas_call | solution.py:329
  159.3 0.0 copy-done
  159.3 3.0 %rows.1 = bf16[8192,128]{1,0:T(8,128)(2,1)} custom-call(s32[1,128]{1,0:T(1,128)S(1)} %copy-done, bf16[128,144,128]{2,1,0:T(8,128)(2,1)S(1)} %levels.1.leafwise), custom_call_target="tpu_custom_call" | custom-call | tf_op jit(solution)/shard_map/rows/pallas_call | solution.py:368
Async XLA Ops:
  0.0 159.3 %copy-start = (s32[1,128]{1,0:T(1,128)S(1)}, s32[1,128]{1,0:T(1,128)}, u32[]{:S(2)}) copy-start(s32[1,128]{1,0:T(1,128)} %sizes.1) | copy-start | bytes 1540

commit v2 on v1

--- a/solution.py
+++ b/solution.py
@@ -188,13 +188,15 @@
             copy.start()
     load_rf.start()
     pl.semaphore_wait(barrier, n)
+    loads(0)[0].wait()
+    weight_copies(0)[0].start()
     hand_out(0, leaves)
 
     for l in range(levels):
-        for copy in loads(l):
+        for copy in loads(l)[l == 0:]:
             copy.wait()
         pack(l)
-        for copy in weight_copies(l):
+        for copy in weight_copies(l)[l == 0:]:
             copy.start()
     load_rf.wait()
 
@@ -208,72 +210,100 @@
 
     blank = jnp.zeros((2 * LANES - width, LANES), bf16)
 
-    def combine(l, par, put):
+    def blend(l, par, s, at, first, second):
+        arrival(par, s).wait_recv()
+        arrival(par, s + half).wait_recv()
+        for q in range(per):
+            i = at * per + q
+            x = arr[par, s, q]
+            y = arr[par, s + half, q]
+            jx = turn(x)
+            jy = turn(y)
+            rest = second[l, i]
+            upper = jnp.concatenate([first[l, 0, i], rest], axis=1)
+            lower = jnp.concatenate([first[l, 1, i], rest], axis=1)
+            cut = LANES - 2 * rank
+            over = jnp.concatenate([x, jx, y, jy, blank], axis=0)
+            under = jnp.concatenate([y, jy, x[:cut], blank, x[cut:], jx], axis=0)
+            coef[s * per + q] = jnp.dot(
+                upper, over, preferred_element_type=jnp.float32
+            ).astype(bf16)
+            coef[(s + half) * per + q] = jnp.dot(
+                lower, under, preferred_element_type=jnp.float32
+            ).astype(bf16)
+
+    def weights_here(l):
+        for copy in weight_copies(l):
+            copy.wait_recv()
+
+    def combine_first(par):
         def pairs(owner, first, second):
             def one(k, inner):
                 at = lax.rem(place + sources - k, sources)
-                s = owner * sources + at
-                arrival(par, s).wait_recv()
-                arrival(par, s + half).wait_recv()
-                for q in range(per):
-                    i = at * per + q
-                    x = arr[par, s, q]
-                    y = arr[par, s + half, q]
-                    jx = turn(x)
-                    jy = turn(y)
-                    rest = second[l, i]
-                    upper = jnp.concatenate([first[l, 0, i], rest], axis=1)
-                    lower = jnp.concatenate([first[l, 1, i], rest], axis=1)
-                    cut = LANES - 2 * rank
-                    over = jnp.concatenate([x, jx, y, jy, blank], axis=0)
-                    under = jnp.concatenate([y, jy, x[:cut], blank, x[cut:], jx], axis=0)
-                    put(s * per + q, jnp.dot(
-                        upper, over, preferred_element_type=jnp.float32
-                    ).astype(bf16))
-                    put((s + half) * per + q, jnp.dot(
-                        lower, under, preferred_element_type=jnp.float32
-                    ).astype(bf16))
+                blend(0, par, owner * sources + at, at, first, second)
                 return inner
 
             lax.fori_loop(0, sources, one, 0)
 
         pairs(col, head, tail)
-        for copy in weight_copies(l):
-            copy.wait_recv()
+        weights_here(0)
         pairs(1 - col, head_in, tail_in)
 
-    def keep_block(b, values):
-        coef[b] = values
-
-    def level(l, carry):
-        par = lax.rem(l, 2)
-        combine(l, par, keep_block)
-
-        @pl.when(l > 0)
-        def _():
-            sent(1 - par)
-
+    def combine(l, par, after=None):
+        weights_here(l)
+
+        def one(k, inner):
+            s = lax.rem(place + half - k, half)
+            at = lax.rem(s, sources)
+            own = s // sources == col
+
+            @pl.when(own)
+            def _():
+                blend(l, par, s, at, head, tail)
+
+            @pl.when(jnp.logical_not(own))
+            def _():
+                blend(l, par, s, at, head_in, tail_in)
+
+            if after is not None:
+                after(s)
+            return inner
+
+        lax.fori_loop(0, half, one, 0)
+
+    def pass_on(l, par):
         def choose(peer):
             for q in range(per):
                 send[1 - par, peer, q] = coef[order[l + 1, peer * per + q]]
 
         hand_out(1 - par, choose)
+
+    combine_first(0)
+    pass_on(0, 0)
+
+    def level(l, carry):
+        par = lax.rem(l, 2)
+        combine(l, par)
+        sent(1 - par)
+        pass_on(l, par)
         return carry
 
-    lax.fori_loop(0, levels - 1, level, 0)
+    lax.fori_loop(1, levels - 1, level, 0)
 
     reach = leafwise.shape[1]
 
-    def put_rows(b, values):
-        base = lax.div(row_start[b], ROWS)
-        rows = [flipped[base + i] for i in range(reach // ROWS)]
-        pair = jnp.concatenate([values, turn(values)], axis=0)
-        leafwise[b] = jnp.dot(
-            jnp.concatenate(rows, axis=0), pair, preferred_element_type=jnp.float32
-        ).astype(bf16)
+    def rows(s):
+        for b in [t * per + q for t in (s, s + half) for q in range(per)]:
+            base = lax.div(row_start[b], ROWS)
+            window = [flipped[base + i] for i in range(reach // ROWS)]
+            values = coef[b]
+            pair = jnp.concatenate([values, turn(values)], axis=0)
+            leafwise[b] = jnp.dot(
+                jnp.concatenate(window, axis=0), pair, preferred_element_type=jnp.float32
+            ).astype(bf16)
 
     last = (levels - 1) % 2
-    combine(levels - 1, last, put_rows)
+    combine(levels - 1, last, rows)
     sent(1 - last)
     sent(last)
     for l in range(levels):
@@ -304,11 +334,13 @@
             out[pl.ds(base + ROWS, reach - ROWS), :] = leafwise[b, pl.ds(ROWS, reach - ROWS), :]
             start = start + sizes[0, b]
 
+        @pl.when(start // chunk > begin // chunk)
+        def _():
+            part(begin // chunk).start()
+
         return start
 
     lax.fori_loop(0, blocks // group, leaves, jnp.int32(0))
-    for c in range(parts):
-        part(c).start()
     for c in range(parts):
         part(c).wait()
 

time: 163 us -> 149 us (0.914)
  Pallas kernels: 162 us -> 149 us
    pallas_call x1, Pallas kernels: 159 us -> 146 us  [local(): pl.pallas_call(functools.partial(main_kernel, n), out_shape=pltpu.VMEM((b...]
where the time goes in v2:
time: 149 us
  Pallas kernels  149 us (100%)
    pallas_call x1, Pallas kernels, local(): pl.pallas_call(functools.partial(main_kernel, n), out_shape=pltpu.VMEM((b...  146 us

profile of v2, /device:TPU:0, one launch (start us, length us, event | category | flops | bytes accessed | tf_op | source)
XLA Modules:
  0.0 149.0 jit_solution(11993963265805753316)
XLA Ops:
  0.0 0.0 copy-start
  0.0 146.5 %levels.1.leafwise = bf16[128,144,128]{2,1,0:T(8,128)(2,1)S(1)} custom-call(bf16[64,128,128]{2,1,0:T(8,128)(2,1)} %bitcast.4, bf16[96,8192]{1,0:T(8,128)(2,1)} %cf_hbm.1, bf16[96,8192]{1,0:T(8,128)(2,1)} %rf_hbm.1, bf16[4,2,32,48,192]{4,3,2,1,0:T(8,128)(2,1)} %bitcast.3, s32[1,128]{1,0:T(1,128)} %col_sizes_hbm.1, s32[1,128]{1,0:T(1,128)} %sizes.1, ...), custom_call_target="tpu_custom_call" | custom-call | tf_op jit(solution)/shard_map/levels/pallas_call | solution.py:361
  146.5 0.0 copy-done
  146.5 2.5 %rows.1 = bf16[8192,128]{1,0:T(8,128)(2,1)} custom-call(s32[1,128]{1,0:T(1,128)S(1)} %copy-done, bf16[128,144,128]{2,1,0:T(8,128)(2,1)S(1)} %levels.1.leafwise), custom_call_target="tpu_custom_call" | custom-call | tf_op jit(solution)/shard_map/rows/pallas_call | solution.py:400
Async XLA Ops:
  0.0 146.5 %copy-start = (s32[1,128]{1,0:T(1,128)S(1)}, s32[1,128]{1,0:T(1,128)}, u32[]{:S(2)}) copy-start(s32[1,128]{1,0:T(1,128)} %sizes.1) | copy-start | bytes 1540

commit v3 on v2

--- a/solution.py
+++ b/solution.py
@@ -19,13 +19,13 @@
 
 def main_kernel(
     n, sig_hbm, cf_hbm, rf_hbm, lf_hbm, col_sizes_hbm, row_sizes_hbm, order_hbm, leafwise,
-    sig, cf, rf, flipped, head, tail, head_in, tail_in, loose, coef, send, arr,
+    sig, cf, rf, flipped, head, tail, head_in, tail_in, loose, mixed, send, arr,
     col_sizes, row_sizes, order, col_start, row_start,
     load_sem, cf_sem, small_sem, w_send, w_recv, a_send, a_recv,
 ):
     levels, _, depth, rank, _ = head.shape
     width = LANES + loose.shape[-1]
-    blocks = coef.shape[0]
+    blocks = mixed.shape[2]
     chunks = sig.shape[0]
     per = blocks // n
     half = n // 2
@@ -110,22 +110,22 @@
 
         lax.fori_loop(0, depth, one, 0, unroll=4)
 
-    def block_copy(par, peer):
+    def block_copy(t, par, peer):
         return pltpu.make_async_remote_copy(
-            src_ref=send.at[par, peer],
-            dst_ref=arr.at[par, me],
-            send_sem=a_send.at[par, peer],
-            recv_sem=a_recv.at[par, me],
+            src_ref=send.at[t, par, peer],
+            dst_ref=arr.at[t, par, me],
+            send_sem=a_send.at[t, par, peer],
+            recv_sem=a_recv.at[t, par, me],
             device_id=(peer, col),
             device_id_type=MESH,
         )
 
-    def arrival(par, source):
+    def arrival(t, par, source):
         return pltpu.make_async_remote_copy(
-            src_ref=send.at[par, source],
-            dst_ref=arr.at[par, source],
-            send_sem=a_send.at[par, source],
-            recv_sem=a_recv.at[par, source],
+            src_ref=send.at[t, par, source],
+            dst_ref=arr.at[t, par, source],
+            send_sem=a_send.at[t, par, source],
+            recv_sem=a_recv.at[t, par, source],
             device_id=(source, col),
             device_id_type=MESH,
         )
@@ -136,33 +136,45 @@
     def beside(k):
         return side * half + lax.rem(place + k, half)
 
-    def hand_out(par, choose):
+    def hand_out(t, par, choose):
         def one(k, inner):
             choose(across(k))
-            block_copy(par, across(k)).start()
+            block_copy(t, par, across(k)).start()
 
             @pl.when(k > 0)
             def _():
                 choose(beside(k))
-                block_copy(par, beside(k)).start()
+                block_copy(t, par, beside(k)).start()
 
             return inner
 
         lax.fori_loop(0, half, one, 0)
         choose(me)
-        pltpu.make_async_copy(send.at[par, me], arr.at[par, me], a_recv.at[par, me]).start()
-
-    def sent(par):
+        pltpu.make_async_copy(
+            send.at[t, par, me], arr.at[t, par, me], a_recv.at[t, par, me]
+        ).start()
+
+    def sent(t, par):
         def one(k, inner):
-            block_copy(par, lax.rem(me + k, n)).wait_send()
+            block_copy(t, par, lax.rem(me + k, n)).wait_send()
             return inner
 
         lax.fori_loop(1, n, one, 0)
+
+    quarter = LANES // 4
+    first_slot = lax.rem(lax.broadcasted_iota(jnp.int32, (rank, LANES), 1), 2 * quarter) < quarter
+
+    def left(values):
+        return pltpu.roll(values, LANES - quarter, 1)
+
+    def right(values):
+        return pltpu.roll(values, quarter, 1)
 
     window = 2 * LANES
     lane = lax.broadcasted_iota(jnp.int32, (1, window), 1)
 
     def leaves(peer):
+        blocks_of = []
         for q in range(per):
             b = order[0, peer * per + q]
             start = col_start[b]
@@ -174,7 +186,11 @@
             weights = jnp.concatenate([cf[c], cf[c + 1]], axis=1) * keep
             values = jnp.concatenate([sig[c], sig[c + 1]], axis=0)
             sums = jnp.dot(weights, values, preferred_element_type=jnp.float32)
-            send[0, peer, q] = (sums[:rank] + turn(sums[rank:])).astype(bf16)
+            blocks_of.append(sums[:rank] + turn(sums[rank:]))
+        for u in range(per // 2):
+            one, two = blocks_of[2 * u], blocks_of[2 * u + 1]
+            send[0, 0, peer, u] = jnp.where(first_slot, one, right(two)).astype(bf16)
+            send[1, 0, peer, u] = jnp.where(first_slot, left(one), two).astype(bf16)
 
     load_sig.wait()
 
@@ -190,7 +206,8 @@
     pl.semaphore_wait(barrier, n)
     loads(0)[0].wait()
     weight_copies(0)[0].start()
-    hand_out(0, leaves)
+    hand_out(0, 0, leaves)
+    hand_out(1, 0, lambda peer: None)
 
     for l in range(levels):
         for copy in loads(l)[l == 0:]:
@@ -210,48 +227,53 @@
 
     blank = jnp.zeros((2 * LANES - width, LANES), bf16)
 
-    def blend(l, par, s, at, first, second):
-        arrival(par, s).wait_recv()
-        arrival(par, s + half).wait_recv()
-        for q in range(per):
-            i = at * per + q
-            x = arr[par, s, q]
-            y = arr[par, s + half, q]
+    def keep(t, j, sums):
+        pair = jnp.where(first_slot, sums[:rank], sums[rank:])
+        both = pair.astype(bf16)
+        mixed[t, 0, j] = both
+        mixed[t, 1, j + 1] = both
+        mixed[t, 0, j + 1] = left(pair).astype(bf16)
+        mixed[t, 1, j] = right(pair).astype(bf16)
+
+    def blend(t, l, par, s, at, first, second):
+        arrival(t, par, s).wait_recv()
+        arrival(t, par, s + half).wait_recv()
+        for u in range(per // 2):
+            i = at * per + 2 * u
+            x = arr[t, par, s, u]
+            y = arr[t, par, s + half, u]
             jx = turn(x)
             jy = turn(y)
-            rest = second[l, i]
-            upper = jnp.concatenate([first[l, 0, i], rest], axis=1)
-            lower = jnp.concatenate([first[l, 1, i], rest], axis=1)
+
+            def weights(h):
+                return jnp.concatenate([
+                    jnp.concatenate([first[l, h, i], second[l, i]], axis=1),
+                    jnp.concatenate([first[l, h, i + 1], second[l, i + 1]], axis=1),
+                ], axis=0)
+
             cut = LANES - 2 * rank
             over = jnp.concatenate([x, jx, y, jy, blank], axis=0)
             under = jnp.concatenate([y, jy, x[:cut], blank, x[cut:], jx], axis=0)
-            coef[s * per + q] = jnp.dot(
-                upper, over, preferred_element_type=jnp.float32
-            ).astype(bf16)
-            coef[(s + half) * per + q] = jnp.dot(
-                lower, under, preferred_element_type=jnp.float32
-            ).astype(bf16)
+            keep(t, s * per + 2 * u, jnp.dot(
+                weights(0), over, preferred_element_type=jnp.float32
+            ))
+            keep(t, (s + half) * per + 2 * u, jnp.dot(
+                weights(1), under, preferred_element_type=jnp.float32
+            ))
 
     def weights_here(l):
         for copy in weight_copies(l):
             copy.wait_recv()
 
-    def combine_first(par):
-        def pairs(owner, first, second):
-            def one(k, inner):
-                at = lax.rem(place + sources - k, sources)
-                blend(0, par, owner * sources + at, at, first, second)
-                return inner
-
-            lax.fori_loop(0, sources, one, 0)
-
-        pairs(col, head, tail)
-        weights_here(0)
-        pairs(1 - col, head_in, tail_in)
-
-    def combine(l, par, after=None):
-        weights_here(l)
-
+    def pairs(t, owner, first, second):
+        def one(k, inner):
+            at = lax.rem(place + sources - k, sources)
+            blend(t, 0, 0, owner * sources + at, at, first, second)
+            return inner
+
+        lax.fori_loop(0, sources, one, 0)
+
+    def combine(t, l, par, after=None):
         def one(k, inner):
             s = lax.rem(place + half - k, half)
             at = lax.rem(s, sources)
@@ -259,11 +281,11 @@
 
             @pl.when(own)
             def _():
-                blend(l, par, s, at, head, tail)
+                blend(t, l, par, s, at, head, tail)
 
             @pl.when(jnp.logical_not(own))
             def _():
-                blend(l, par, s, at, head_in, tail_in)
+                blend(t, l, par, s, at, head_in, tail_in)
 
             if after is not None:
                 after(s)
@@ -271,21 +293,30 @@
 
         lax.fori_loop(0, half, one, 0)
 
-    def pass_on(l, par):
+    def pass_on(t, l, par):
         def choose(peer):
-            for q in range(per):
-                send[1 - par, peer, q] = coef[order[l + 1, peer * per + q]]
-
-        hand_out(1 - par, choose)
-
-    combine_first(0)
-    pass_on(0, 0)
+            for u in range(per // 2):
+                one = order[l + 1, peer * per + 2 * u]
+                two = order[l + 1, peer * per + 2 * u + 1]
+                send[t, 1 - par, peer, u] = jnp.where(first_slot, mixed[t, 0, one], mixed[t, 1, two])
+
+        hand_out(t, 1 - par, choose)
+
+    pairs(0, col, head, tail)
+    weights_here(0)
+    pairs(0, 1 - col, head_in, tail_in)
+    pass_on(0, 0, 0)
+    pairs(1, col, head, tail)
+    pairs(1, 1 - col, head_in, tail_in)
+    pass_on(1, 0, 0)
 
     def level(l, carry):
         par = lax.rem(l, 2)
-        combine(l, par)
-        sent(1 - par)
-        pass_on(l, par)
+        weights_here(l)
+        for t in range(2):
+            combine(t, l, par)
+            sent(t, 1 - par)
+            pass_on(t, l, par)
         return carry
 
     lax.fori_loop(1, levels - 1, level, 0)
@@ -296,16 +327,19 @@
         for b in [t * per + q for t in (s, s + half) for q in range(per)]:
             base = lax.div(row_start[b], ROWS)
             window = [flipped[base + i] for i in range(reach // ROWS)]
-            values = coef[b]
+            values = jnp.where(first_slot, mixed[0, 0, b], mixed[1, 1, b])
             pair = jnp.concatenate([values, turn(values)], axis=0)
             leafwise[b] = jnp.dot(
                 jnp.concatenate(window, axis=0), pair, preferred_element_type=jnp.float32
             ).astype(bf16)
 
     last = (levels - 1) % 2
-    combine(levels - 1, last, rows)
-    sent(1 - last)
-    sent(last)
+    weights_here(levels - 1)
+    combine(0, levels - 1, last)
+    combine(1, levels - 1, last, rows)
+    for t in range(2):
+        sent(t, 1 - last)
+        sent(t, last)
     for l in range(levels):
         for copy in weight_copies(l):
             copy.wait_send()
@@ -373,9 +407,9 @@
             pltpu.VMEM((levels, halves, depth, rank, LANES), bf16),
             pltpu.VMEM((levels, depth, rank, LANES), bf16),
             pltpu.VMEM((levels, halves, depth, rank, width - LANES), bf16),
-            pltpu.VMEM((blocks, rank, columns), bf16),
-            pltpu.VMEM((2, n, per, rank, columns), bf16),
-            pltpu.VMEM((2, n, per, rank, columns), bf16),
+            pltpu.VMEM((2, 2, blocks, rank, columns), bf16),
+            pltpu.VMEM((2, 2, n, per // 2, rank, columns), bf16),
+            pltpu.VMEM((2, 2, n, per // 2, rank, columns), bf16),
             pltpu.SMEM((1, blocks), jnp.int32),
             pltpu.SMEM((1, blocks), jnp.int32),
             pltpu.SMEM((levels, blocks), jnp.int32),
@@ -386,8 +420,8 @@
             pltpu.SemaphoreType.DMA((3,)),
             pltpu.SemaphoreType.DMA((levels, 2)),
             pltpu.SemaphoreType.DMA((levels, 2)),
-            pltpu.SemaphoreType.DMA((2, n)),
-            pltpu.SemaphoreType.DMA((2, n)),
+            pltpu.SemaphoreType.DMA((2, 2, n)),
+            pltpu.SemaphoreType.DMA((2, 2, n)),
         ],
         compiler_params=pltpu.CompilerParams(
             collective_id=0, has_side_effects=True, vmem_limit_bytes=58000000
@@ -404,7 +438,7 @@
         out_specs=hbm,
         scratch_shapes=[
             pltpu.VMEM((points + reach, columns), bf16),
-            pltpu.SemaphoreType.DMA((8,)),
+            pltpu.SemaphoreType.DMA((points // (8 * LANES),)),
         ],
         compiler_params=pltpu.CompilerParams(vmem_limit_bytes=16 << 20),
         name="rows",

time: 149 us -> 151 us (1.013)
  Pallas kernels: 149 us -> 151 us
    pallas_call x1, Pallas kernels: 146 us -> 148 us  [local(): pl.pallas_call(functools.partial(main_kernel, n), out_shape=pltpu.VMEM((b...]
where the time goes in v3:
time: 151 us
  Pallas kernels  151 us (100%)
    pallas_call x1, Pallas kernels, local(): pl.pallas_call(functools.partial(main_kernel, n), out_shape=pltpu.VMEM((b...  148 us

profile of v3, /device:TPU:0, one launch (start us, length us, event | category | flops | bytes accessed | tf_op | source)
XLA Modules:
  0.0 151.0 jit_solution(2061131802843572600)
XLA Ops:
  0.0 0.0 copy-start
  0.0 148.5 %levels.1.leafwise = bf16[128,144,128]{2,1,0:T(8,128)(2,1)S(1)} custom-call(bf16[64,128,128]{2,1,0:T(8,128)(2,1)} %bitcast.4, bf16[96,8192]{1,0:T(8,128)(2,1)} %cf_hbm.1, bf16[96,8192]{1,0:T(8,128)(2,1)} %rf_hbm.1, bf16[4,2,32,48,192]{4,3,2,1,0:T(8,128)(2,1)} %bitcast.3, s32[1,128]{1,0:T(1,128)} %col_sizes_hbm.1, s32[1,128]{1,0:T(1,128)} %sizes.1, ...), custom_call_target="tpu_custom_call" | custom-call | tf_op jit(solution)/shard_map/levels/pallas_call | solution.py:395
  148.5 0.0 copy-done
  148.5 2.5 %rows.1 = bf16[8192,128]{1,0:T(8,128)(2,1)} custom-call(s32[1,128]{1,0:T(1,128)S(1)} %copy-done, bf16[128,144,128]{2,1,0:T(8,128)(2,1)S(1)} %levels.1.leafwise), custom_call_target="tpu_custom_call" | custom-call | tf_op jit(solution)/shard_map/rows/pallas_call | solution.py:434
Async XLA Ops:
  0.0 148.5 %copy-start = (s32[1,128]{1,0:T(1,128)S(1)}, s32[1,128]{1,0:T(1,128)}, u32[]{:S(2)}) copy-start(s32[1,128]{1,0:T(1,128)} %sizes.1) | copy-start | bytes 1540

commit v4 on v2

--- a/solution.py
+++ b/solution.py
@@ -45,7 +45,7 @@
 
     def load_cf(c):
         at = pl.ds(pl.multiple_of(c * LANES, LANES), LANES)
-        return pltpu.make_async_copy(cf_hbm.at[:, at], cf.at[c], cf_sem.at[c])
+        return pltpu.make_async_copy(cf_hbm.at[:, at], cf.at[c], cf_sem)
 
     load_rf = pltpu.make_async_copy(rf_hbm, rf, load_sem.at[levels, 2])
 
@@ -114,7 +114,7 @@
         return pltpu.make_async_remote_copy(
             src_ref=send.at[par, peer],
             dst_ref=arr.at[par, me],
-            send_sem=a_send.at[par, peer],
+            send_sem=a_send.at[par],
             recv_sem=a_recv.at[par, me],
             device_id=(peer, col),
             device_id_type=MESH,
@@ -124,7 +124,7 @@
         return pltpu.make_async_remote_copy(
             src_ref=send.at[par, source],
             dst_ref=arr.at[par, source],
-            send_sem=a_send.at[par, source],
+            send_sem=a_send.at[par],
             recv_sem=a_recv.at[par, source],
             device_id=(source, col),
             device_id_type=MESH,
@@ -153,11 +153,8 @@
         pltpu.make_async_copy(send.at[par, me], arr.at[par, me], a_recv.at[par, me]).start()
 
     def sent(par):
-        def one(k, inner):
-            block_copy(par, lax.rem(me + k, n)).wait_send()
-            return inner
-
-        lax.fori_loop(1, n, one, 0)
+        gone = send.at[par, pl.ds(0, n - 1)]
+        pltpu.make_async_copy(gone, gone, a_send.at[par]).wait()
 
     window = 2 * LANES
     lane = lax.broadcasted_iota(jnp.int32, (1, window), 1)
@@ -178,11 +175,7 @@
 
     load_sig.wait()
 
-    def wait_cf(c, carry):
-        load_cf(c).wait()
-        return carry
-
-    lax.fori_loop(0, chunks, wait_cf, 0)
+    pltpu.make_async_copy(cf, cf, cf_sem).wait()
     for l in range(levels):
         for copy in loads(l):
             copy.start()
@@ -382,11 +375,11 @@
             pltpu.SMEM((blocks,), jnp.int32),
             pltpu.SMEM((blocks,), jnp.int32),
             pltpu.SemaphoreType.DMA((levels + 1, 3)),
-            pltpu.SemaphoreType.DMA((points // LANES,)),
+            pltpu.SemaphoreType.DMA(()),
             pltpu.SemaphoreType.DMA((3,)),
             pltpu.SemaphoreType.DMA((levels, 2)),
             pltpu.SemaphoreType.DMA((levels, 2)),
-            pltpu.SemaphoreType.DMA((2, n)),
+            pltpu.SemaphoreType.DMA((2,)),
             pltpu.SemaphoreType.DMA((2, n)),
         ],
         compiler_params=pltpu.CompilerParams(
@@ -404,7 +397,7 @@
         out_specs=hbm,
         scratch_shapes=[
             pltpu.VMEM((points + reach, columns), bf16),
-            pltpu.SemaphoreType.DMA((8,)),
+            pltpu.SemaphoreType.DMA((points // (8 * LANES),)),
         ],
         compiler_params=pltpu.CompilerParams(vmem_limit_bytes=16 << 20),
         name="rows",

time: 149 us -> 148 us (level)
  no operation moved by 1% of the time
where the time goes in v4:
time: 148 us
  Pallas kernels  148 us (100%)
    pallas_call x1, Pallas kernels, local(): pl.pallas_call(functools.partial(main_kernel, n), out_shape=pltpu.VMEM((b...  145 us

profile of v4, /device:TPU:0, one launch (start us, length us, event | category | flops | bytes accessed | tf_op | source)
XLA Modules:
  0.0 147.8 jit_solution(8995397286713995817)
XLA Ops:
  0.0 0.0 copy-start
  0.0 145.3 %levels.1.leafwise = bf16[128,144,128]{2,1,0:T(8,128)(2,1)S(1)} custom-call(bf16[64,128,128]{2,1,0:T(8,128)(2,1)} %bitcast.4, bf16[96,8192]{1,0:T(8,128)(2,1)} %cf_hbm.1, bf16[96,8192]{1,0:T(8,128)(2,1)} %rf_hbm.1, bf16[4,2,32,48,192]{4,3,2,1,0:T(8,128)(2,1)} %bitcast.3, s32[1,128]{1,0:T(1,128)} %col_sizes_hbm.1, s32[1,128]{1,0:T(1,128)} %sizes.1, ...), custom_call_target="tpu_custom_call" | custom-call | tf_op jit(solution)/shard_map/levels/pallas_call | solution.py:354
  145.3 0.0 copy-done
  145.3 2.5 %rows.1 = bf16[8192,128]{1,0:T(8,128)(2,1)} custom-call(s32[1,128]{1,0:T(1,128)S(1)} %copy-done, bf16[128,144,128]{2,1,0:T(8,128)(2,1)S(1)} %levels.1.leafwise), custom_call_target="tpu_custom_call" | custom-call | tf_op jit(solution)/shard_map/rows/pallas_call | solution.py:393
Async XLA Ops:
  0.0 145.3 %copy-start = (s32[1,128]{1,0:T(1,128)S(1)}, s32[1,128]{1,0:T(1,128)}, u32[]{:S(2)}) copy-start(s32[1,128]{1,0:T(1,128)} %sizes.1) | copy-start | bytes 1540

commit v5 on v4

--- a/solution.py
+++ b/solution.py
@@ -41,33 +41,25 @@
         pltpu.make_async_copy(order_hbm, order, small_sem.at[1]),
         pltpu.make_async_copy(row_sizes_hbm, row_sizes, small_sem.at[2]),
     ]
-    load_sig = pltpu.make_async_copy(sig_hbm, sig, load_sem.at[levels, 0])
+    load_sig = pltpu.make_async_copy(sig_hbm, sig, load_sem.at[0])
 
     def load_cf(c):
         at = pl.ds(pl.multiple_of(c * LANES, LANES), LANES)
         return pltpu.make_async_copy(cf_hbm.at[:, at], cf.at[c], cf_sem)
 
-    load_rf = pltpu.make_async_copy(rf_hbm, rf, load_sem.at[levels, 2])
-
-    def loads(l):
-        return (
-            pltpu.make_async_copy(
-                lf_hbm.at[l, :, :, :, pl.ds(0, LANES)], head.at[l], load_sem.at[l, 0]
-            ),
-            pltpu.make_async_copy(
-                lf_hbm.at[l, :, :, :, pl.ds(LANES, width - LANES)], loose.at[l], load_sem.at[l, 1]
-            ),
-        )
-
-    for copy in smalls:
-        copy.start()
-    load_sig.start()
-
-    def start_cf(c, carry):
-        load_cf(c).start()
-        return carry
-
-    lax.fori_loop(0, chunks, start_cf, 0)
+    load_rf = pltpu.make_async_copy(rf_hbm, rf, load_sem.at[1])
+
+    tops = pl.ds(0, LANES)
+    load_head = pltpu.make_async_copy(
+        lf_hbm.at[0, :, :, :, tops], head.at[0], load_sem.at[2]
+    )
+    later = pl.ds(1, levels - 1)
+    load_heads = pltpu.make_async_copy(
+        lf_hbm.at[later, :, :, :, tops], head.at[later], load_sem.at[3]
+    )
+    load_loose = pltpu.make_async_copy(
+        lf_hbm.at[:, :, :, :, pl.ds(LANES, width - LANES)], loose, load_sem.at[4]
+    )
 
     barrier = pltpu.get_barrier_semaphore()
 
@@ -78,6 +70,16 @@
 
     lax.fori_loop(1, n, greet, 0)
     pl.semaphore_signal(barrier, inc=1, device_id=(me, 1 - col), device_id_type=MESH)
+
+    for copy in smalls:
+        copy.start()
+    load_sig.start()
+
+    def start_cf(c, carry):
+        load_cf(c).start()
+        return carry
+
+    lax.fori_loop(0, chunks, start_cf, 0)
 
     for copy in smalls:
         copy.wait()
@@ -90,18 +92,21 @@
 
     lax.fori_loop(0, blocks, add_up, (jnp.int32(0), jnp.int32(0)), unroll=8)
 
-    def weight_copies(l):
-        return [
-            pltpu.make_async_remote_copy(
-                src_ref=ref.at[l],
-                dst_ref=into.at[l],
-                send_sem=w_send.at[l, at],
-                recv_sem=w_recv.at[l, at],
-                device_id=(me, 1 - col),
-                device_id_type=MESH,
-            )
-            for at, (ref, into) in enumerate(((head, head_in), (tail, tail_in)))
-        ]
+    def weight_copy(l, at, ref, into):
+        return pltpu.make_async_remote_copy(
+            src_ref=ref.at[l],
+            dst_ref=into.at[l],
+            send_sem=w_send.at[at],
+            recv_sem=w_recv.at[l, at],
+            device_id=(me, 1 - col),
+            device_id_type=MESH,
+        )
+
+    def head_copy(l):
+        return weight_copy(l, 0, head, head_in)
+
+    def tail_copy(l):
+        return weight_copy(l, 1, tail, tail_in)
 
     def pack(l):
         def one(i, carry):
@@ -138,14 +143,13 @@
 
     def hand_out(par, choose):
         def one(k, inner):
-            choose(across(k))
-            block_copy(par, across(k)).start()
-
             @pl.when(k > 0)
             def _():
                 choose(beside(k))
                 block_copy(par, beside(k)).start()
 
+            choose(across(k))
+            block_copy(par, across(k)).start()
             return inner
 
         lax.fori_loop(0, half, one, 0)
@@ -176,21 +180,23 @@
     load_sig.wait()
 
     pltpu.make_async_copy(cf, cf, cf_sem).wait()
-    for l in range(levels):
-        for copy in loads(l):
-            copy.start()
+    load_head.start()
+    load_loose.start()
+    load_heads.start()
     load_rf.start()
     pl.semaphore_wait(barrier, n)
-    loads(0)[0].wait()
-    weight_copies(0)[0].start()
+    load_head.wait()
+    head_copy(0).start()
     hand_out(0, leaves)
 
-    for l in range(levels):
-        for copy in loads(l)[l == 0:]:
-            copy.wait()
+    load_loose.wait()
+    pack(0)
+    tail_copy(0).start()
+    load_heads.wait()
+    for l in range(1, levels):
+        head_copy(l).start()
         pack(l)
-        for copy in weight_copies(l)[l == 0:]:
-            copy.start()
+        tail_copy(l).start()
     load_rf.wait()
 
     def flip(c, inner):
@@ -226,21 +232,8 @@
             ).astype(bf16)
 
     def weights_here(l):
-        for copy in weight_copies(l):
-            copy.wait_recv()
-
-    def combine_first(par):
-        def pairs(owner, first, second):
-            def one(k, inner):
-                at = lax.rem(place + sources - k, sources)
-                blend(0, par, owner * sources + at, at, first, second)
-                return inner
-
-            lax.fori_loop(0, sources, one, 0)
-
-        pairs(col, head, tail)
-        weights_here(0)
-        pairs(1 - col, head_in, tail_in)
+        head_copy(l).wait_recv()
+        tail_copy(l).wait_recv()
 
     def combine(l, par, after=None):
         weights_here(l)
@@ -271,17 +264,18 @@
 
         hand_out(1 - par, choose)
 
-    combine_first(0)
-    pass_on(0, 0)
-
     def level(l, carry):
         par = lax.rem(l, 2)
         combine(l, par)
-        sent(1 - par)
+
+        @pl.when(l > 0)
+        def _():
+            sent(1 - par)
+
         pass_on(l, par)
         return carry
 
-    lax.fori_loop(1, levels - 1, level, 0)
+    lax.fori_loop(0, levels - 1, level, 0)
 
     reach = leafwise.shape[1]
 
@@ -299,9 +293,8 @@
     combine(levels - 1, last, rows)
     sent(1 - last)
     sent(last)
-    for l in range(levels):
-        for copy in weight_copies(l):
-            copy.wait_send()
+    pltpu.make_async_copy(head, head, w_send.at[0]).wait()
+    pltpu.make_async_copy(tail, tail, w_send.at[1]).wait()
 
 
 def rows_kernel(sizes, leafwise, out_hbm, out, sem):
@@ -374,10 +367,10 @@
             pltpu.SMEM((levels, blocks), jnp.int32),
             pltpu.SMEM((blocks,), jnp.int32),
             pltpu.SMEM((blocks,), jnp.int32),
-            pltpu.SemaphoreType.DMA((levels + 1, 3)),
+            pltpu.SemaphoreType.DMA((5,)),
             pltpu.SemaphoreType.DMA(()),
             pltpu.SemaphoreType.DMA((3,)),
-            pltpu.SemaphoreType.DMA((levels, 2)),
+            pltpu.SemaphoreType.DMA((2,)),
             pltpu.SemaphoreType.DMA((levels, 2)),
             pltpu.SemaphoreType.DMA((2,)),
             pltpu.SemaphoreType.DMA((2, n)),

time: 148 us -> 148 us (level)
  no operation moved by 1% of the time
where the time goes in v5:
time: 148 us; the launch traced here: 147 us
  Pallas kernels  147 us (99%)
    pallas_call x1, Pallas kernels, local(): pl.pallas_call(functools.partial(main_kernel, n), out_shape=pltpu.VMEM((b...  144 us

profile of v5, /device:TPU:0, one launch (start us, length us, event | category | flops | bytes accessed | tf_op | source)
XLA Modules:
  0.0 147.0 jit_solution(15021098842661008914)
XLA Ops:
  0.0 0.0 copy-start
  0.0 144.5 %levels.1.leafwise = bf16[128,144,128]{2,1,0:T(8,128)(2,1)S(1)} custom-call(bf16[64,128,128]{2,1,0:T(8,128)(2,1)} %bitcast.4, bf16[96,8192]{1,0:T(8,128)(2,1)} %cf_hbm.1, bf16[96,8192]{1,0:T(8,128)(2,1)} %rf_hbm.1, bf16[4,2,32,48,192]{4,3,2,1,0:T(8,128)(2,1)} %bitcast.3, s32[1,128]{1,0:T(1,128)} %col_sizes_hbm.1, s32[1,128]{1,0:T(1,128)} %sizes.1, ...), custom_call_target="tpu_custom_call" | custom-call | tf_op jit(solution)/shard_map/levels/pallas_call | solution.py:347
  144.5 0.0 copy-done
  144.5 2.5 %rows.1 = bf16[8192,128]{1,0:T(8,128)(2,1)} custom-call(s32[1,128]{1,0:T(1,128)S(1)} %copy-done, bf16[128,144,128]{2,1,0:T(8,128)(2,1)S(1)} %levels.1.leafwise), custom_call_target="tpu_custom_call" | custom-call | tf_op jit(solution)/shard_map/rows/pallas_call | solution.py:386
Async XLA Ops:
  0.0 144.5 %copy-start = (s32[1,128]{1,0:T(1,128)S(1)}, s32[1,128]{1,0:T(1,128)}, u32[]{:S(2)}) copy-start(s32[1,128]{1,0:T(1,128)} %sizes.1) | copy-start | bytes 1540

commit v6 on v5

--- a/solution.py
+++ b/solution.py
@@ -141,14 +141,17 @@
     def beside(k):
         return side * half + lax.rem(place + k, half)
 
-    def hand_out(par, choose):
+    def hand_out(par, choose, chosen=0):
         def one(k, inner):
             @pl.when(k > 0)
             def _():
                 choose(beside(k))
                 block_copy(par, beside(k)).start()
 
-            choose(across(k))
+            @pl.when(k >= chosen)
+            def _():
+                choose(across(k))
+
             block_copy(par, across(k)).start()
             return inner
 
@@ -184,10 +187,12 @@
     load_loose.start()
     load_heads.start()
     load_rf.start()
+    leaves(across(0))
+    leaves(across(1))
+    load_head.wait()
     pl.semaphore_wait(barrier, n)
-    load_head.wait()
     head_copy(0).start()
-    hand_out(0, leaves)
+    hand_out(0, leaves, 2)
 
     load_loose.wait()
     pack(0)

time: 148 us -> 147 us (level)
  no operation moved by 1% of the time
where the time goes in v6:
time: 147 us
  Pallas kernels  146 us (99%)
    pallas_call x1, Pallas kernels, local(): pl.pallas_call(functools.partial(main_kernel, n), out_shape=pltpu.VMEM((b...  144 us

profile of v6, /device:TPU:0, one launch (start us, length us, event | category | flops | bytes accessed | tf_op | source)
XLA Modules:
  0.0 146.5 jit_solution(361148185906836638)
XLA Ops:
  0.0 0.0 copy-start
  0.0 144.0 %levels.1.leafwise = bf16[128,144,128]{2,1,0:T(8,128)(2,1)S(1)} custom-call(bf16[64,128,128]{2,1,0:T(8,128)(2,1)} %bitcast.4, bf16[96,8192]{1,0:T(8,128)(2,1)} %cf_hbm.1, bf16[96,8192]{1,0:T(8,128)(2,1)} %rf_hbm.1, bf16[4,2,32,48,192]{4,3,2,1,0:T(8,128)(2,1)} %bitcast.3, s32[1,128]{1,0:T(1,128)} %col_sizes_hbm.1, s32[1,128]{1,0:T(1,128)} %sizes.1, ...), custom_call_target="tpu_custom_call" | custom-call | tf_op jit(solution)/shard_map/levels/pallas_call | solution.py:352
  144.0 0.0 copy-done
  144.0 2.5 %rows.1 = bf16[8192,128]{1,0:T(8,128)(2,1)} custom-call(s32[1,128]{1,0:T(1,128)S(1)} %copy-done, bf16[128,144,128]{2,1,0:T(8,128)(2,1)S(1)} %levels.1.leafwise), custom_call_target="tpu_custom_call" | custom-call | tf_op jit(solution)/shard_map/rows/pallas_call | solution.py:391
Async XLA Ops:
  0.0 144.0 %copy-start = (s32[1,128]{1,0:T(1,128)S(1)}, s32[1,128]{1,0:T(1,128)}, u32[]{:S(2)}) copy-start(s32[1,128]{1,0:T(1,128)} %sizes.1) | copy-start | bytes 1540
